TPU v7x, 256 devices: a whole 4x4x8 slice. The times are simulated.
256 devices in a mesh: panel: 32 (over y, x, core), samp: 8 (over z).
Axes of the slice: x: 4, y: 4, z: 8, core: 2. Of those that a mesh axis runs over, the one named last changes fastest.
Arguments:
- called_allele_tallies: int32 [4096, 1024], P('samp'), may hold values from 0 to 2
- presence_flags: int32 [4096, 1024], P('samp'), may hold values 0 or 1
- reference_panel_strands: int32 [65536, 1024], P('panel'), may hold values from 0 to 1
- softmax_sharpness: float32 [4096], P('samp'), may hold values from 0.02 to 4
- trait_measurements: float32 [4096], P('samp'), may hold values from -8 to 8
- cohort_membership: int32 [4096], P('samp'), may hold values from 0 to 7, as said below
Outputs:
- dosage_out: bfloat16 [4096, 1024], P('samp', 'panel')
- zscore: float32 [1024], P('panel')
Inputs may be any that keep to these rules, and one draw needn't show every extreme that they name: `cohort_membership`: every group id from 0 to 7 occurs.
All inputs are finite; a program needn't handle non-finite values. No bound on the sum of `presence_flags` on one device may be relied on, other than what follows from the above.
Results may differ from a plain program's by a relative error of at most 0.0055.
Values sent between devices are 32-bit elements; how exact they have to be, the bound alone decides.
No kernel may reach another device: no remote copies, remote signals or barrier semaphores. Data moves between devices by JAX's collectives and lax.ppermute only.
A program may use at most 64 MiB of HBM per device.

v0:
```python
import jax
import jax.numpy as jnp
from jax import lax
from jax.sharding import Mesh
from jax.sharding import PartitionSpec as P

GROUPS = 8
PANEL = ("panel_0", "panel_1", "panel_2")
log_two = 0.6931471805599453


def copy_for_each(shard, axis):
    count = lax.axis_size(axis)
    return lax.all_to_all(
        jnp.broadcast_to(shard[None], (count, *shard.shape)), axis, 0, 0, tiled=True
    )


def of_everyone(shard, axis):
    return copy_for_each(shard, axis).sum(axis=0)


def over_copies(shard, axis):
    return copy_for_each(shard, axis).max(axis=0)


def over_axes(shard, axes):
    for axis in axes:
        shard = lax.psum(shard, axis)
    return shard


def in_blocks(shard, dim, count):
    before, after = (shard.shape[:dim], shard.shape[dim + 1 :])
    return jnp.moveaxis(shard.reshape(*before, count, -1, *after), dim, 0)


def sent_and_summed(shard, axis, dim):
    count = lax.axis_size(axis)
    pieces = lax.all_to_all(in_blocks(shard, dim, count), axis, 0, 0, tiled=True)
    return jnp.sum(pieces, axis=0)


def together(arrays, axis):
    line, at, gathered = (jnp.concatenate([a.reshape(-1) for a in arrays]), 0, [])
    so_far = of_everyone(line, axis)
    for a in arrays:
        gathered.append(so_far[at : at + a.size].reshape(a.shape))
        at += a.size
    return tuple(gathered)


def on_device(
    called_allele_tallies,
    presence_flags,
    reference_panel_strands,
    softmax_sharpness,
    trait_measurements,
    cohort_membership,
):
    panel_count = lax.axis_size(PANEL)
    sample_rows, variants = called_allele_tallies.shape
    local_haps = reference_panel_strands.shape[0]
    hap_float = reference_panel_strands.astype(jnp.float32)
    allele_counts = of_everyone(jnp.sum(hap_float, axis=0), PANEL)
    allele_freq = allele_counts / float(local_haps * panel_count)
    geno_float = called_allele_tallies.astype(jnp.float32)
    observed_f = presence_flags.astype(jnp.float32)
    demeaned_expected_count = (observed_f * (geno_float - 2.0 * allele_freq[None, :])).astype(
        jnp.bfloat16
    )
    tile_first_entry = jnp.sum(
        demeaned_expected_count.astype(jnp.float32) * allele_freq[None, :], axis=1
    )
    hap_bf = reference_panel_strands.astype(jnp.bfloat16)
    raw_efficient_statistic = lax.dot_general(
        demeaned_expected_count,
        hap_bf,
        (((1,), (1,)), ((), ())),
        preferred_element_type=jnp.float32,
    )
    panel_match_energies = softmax_sharpness[:, None] * (
        raw_efficient_statistic - tile_first_entry[:, None]
    )
    local_steps = jnp.ceil(jnp.max(panel_match_energies, axis=1) / log_two)
    share = variants // panel_count
    first_column = lax.axis_index(PANEL) * share
    peak_steps = over_copies(local_steps, PANEL)
    weights = jnp.exp(panel_match_energies - log_two * peak_steps[:, None])
    weight_total = over_axes(jnp.sum(weights, axis=1), PANEL)
    partial_dose = 2.0 * jnp.dot(
        weights.astype(jnp.bfloat16), hap_bf, preferred_element_type=jnp.float32
    )
    own_dose = sent_and_summed(partial_dose, PANEL, 1)
    expected_allele_count = own_dose / weight_total[:, None]
    own_geno = lax.dynamic_slice_in_dim(geno_float, first_column, share, 1)
    own_observed = lax.dynamic_slice_in_dim(presence_flags, first_column, share, 1)
    dosage = jnp.where(own_observed == 1, own_geno, expected_allele_count)
    dosage_out = dosage.astype(jnp.bfloat16)
    member = (cohort_membership[:, None] == jnp.arange(GROUPS, dtype=jnp.int32)[None, :]).astype(
        jnp.float32
    )
    group_sum_local = jnp.dot(trait_measurements, member, precision=lax.Precision.HIGHEST)
    group_count_local = jnp.sum(member, axis=0)
    dose_sum_local = jnp.sum(dosage, axis=0)
    dose_square_local = jnp.sum(dosage * dosage, axis=0)
    all_samples = float(sample_rows * lax.axis_size("samp"))
    local_cross = jnp.dot(trait_measurements, dosage, precision=lax.Precision.HIGHEST)
    local_group_dose = jnp.dot(member.T, dosage, precision=lax.Precision.HIGHEST)
    cross, group_dose, dose_sum, dose_square, group_sum, group_count, pheno_square = together(
        (
            local_cross,
            local_group_dose,
            dose_sum_local,
            dose_square_local,
            group_sum_local,
            group_count_local,
            jnp.sum(trait_measurements * trait_measurements),
        ),
        "samp",
    )
    group_mean = group_sum / group_count
    score_u = cross - jnp.dot(group_mean, group_dose, precision=lax.Precision.HIGHEST)
    resid_square = pheno_square - jnp.sum(group_sum * group_mean)
    sigma = resid_square / (all_samples - GROUPS)
    dose_mean = dose_sum / all_samples
    spread = dose_square / all_samples - dose_mean * dose_mean
    zscore = score_u / jnp.sqrt(sigma * all_samples * (spread + 1e-05))
    return (dosage_out, zscore)


def solution(mesh):
    finer = Mesh(
        mesh.devices.reshape(4, 4, 2, mesh.shape["samp"]), ("panel_0", "panel_1", "panel_2", "samp")
    )
    placed = (P("samp", None), P("samp", None), P(PANEL, None), P("samp"), P("samp"), P("samp"))
    return jax.shard_map(
        on_device,
        mesh=finer,
        in_specs=placed,
        out_specs=(P("samp", PANEL), P(PANEL)),
        check_vma=False,
    )
```

profile of v0, /device:TPU:1, one launch (start us, length us, event | category | flops | bytes accessed | tf_op | source)
XLA Modules:
  0.0 123.2 jit_solution(13171496174605333055)
XLA Ops:
  0.6 4.2 %convert_reduce_fusion = f32[1024]{0:T(1024)S(1)} fusion(s32[2048,1024]{1,0:T(8,128)} %param.8), kind=kLoop, calls=%fused_computation | loop fusion | flops 4193280 | bytes 8392704 | tf_op jit(solution)/shard_map/reduce_sum | solution.py:65
  4.8 0.7 broadcast_in_dim.6
  5.5 8.6 %all-to-all-start = ((f32[32,1,1024]{2,1,0:T(1,128)}), f32[32,1,1024]{2,1,0:T(1,128)S(1)}, u32[]{:S(2)}, u32[]{:S(2)}) async-start(f32[32,1,1024]{2,1,0:T(1,128)} %broadcast_in_dim.6), calls=%async_computation | async-start | bytes 262144 | tf_op jit(solution)/shard_map/all_to_all | solution.py:14
  14.1 1.9 %copy.19 = s32[512,1024]{0,1:T(8,128)} copy(s32[512,1024]{1,0:T(8,128)S(1)} %copy-done) | data formatting | bytes 4194304 | tf_op args[1]
  16.0 1.9 %copy.20 = s32[512,1024]{0,1:T(8,128)S(1)} copy(s32[512,1024]{1,0:T(8,128)} %param.6) | data formatting | bytes 4194304 | tf_op args[0]
  17.9 3.8 %all-to-all-done = f32[32,1,1024]{2,1,0:T(1,128)S(1)} async-done(((f32[32,1,1024]{2,1,0:T(1,128)}), f32[32,1,1024]{2,1,0:T(1,128)S(1)}, u32[]{:S(2)}, u32[]{:S(2)}) %all-to-all-start) | async-done | bytes 131104 | tf_op jit(solution)/shard_map/all_to_all | solution.py:14
  21.8 2.1 %multiply_reduce_fusion = (f32[512]{0:T(512)S(1)}, bf16[512,1024]{0,1:T(8,128)(2,1)S(1)}) fusion(f32[1024]{0:T(1024)S(1)} %get-tuple-element.8, f32[1024]{0:T(1024)S(1)} %get-tuple-element.7, s32[512,1024]{0,1:T(8,128)S(1)} %copy.20, s32[512,1024]{0,1:T(8,128)} %copy.19), kind=kLoop, calls=%fused_computation.9 | loop fusion | flops 4193792 | bytes 5253120 | tf_op jit(solution)/shard_map/reduce_sum | solution.py:72
  23.9 7.9 %fusion = (f32[512]{0:T(512)S(1)}, f32[512,2048]{1,0:T(8,128)}) fusion(f32[512]{0:T(512)S(1)} %get-tuple-element.5, f32[512]{0:T(512)S(1)} %copy-done.3, bf16[512,1024]{0,1:T(8,128)(2,1)S(1)} %get-tuple-element.6, s32[2048,1024]{1,0:T(8,128)} %param.8), kind=kOutput, calls=%fused_computation.3 | convolution fusion | flops 2152726016 | bytes 13637632 | tf_op jit(solution)/shard_map/dot_general | solution.py:76
  31.9 11.0 %all_to_all.23 = f32[32,1,512]{2,1,0:T(1,128)S(1)} all-to-all(f32[32,1,512]{2,1,0:T(1,128)S(1)} %broadcast_in_dim.7), channel_id=1, replica_groups=mesh['panel_0'=4,'panel_1'=4,'panel_2'=2,'samp'=8] {'panel_0','panel_1',..., dimensions={0} | all-to-all | bytes 131072 | tf_op jit(solution)/shard_map/all_to_all | solution.py:14
  42.9 8.5 %fusion.11 = f32[512,1024]{1,0:T(8,128)} fusion(s32[2048,1024]{1,0:T(8,128)} %param.8, f32[512,2048]{1,0:T(8,128)} %get-tuple-element.10, f32[512]{0:T(512)S(1)} %broadcast_multiply_fusion.2, f32[512]{0:T(512)S(1)} %get-tuple-element.5, f32[512]{0:T(512)S(1)} %copy-done.3), kind=kOutput, calls=%fused_computation.15 | convolution fusion | flops 2154299392 | bytes 14686208 | tf_op jit(solution)/shard_map/dot_general | solution.py:91
  51.4 2.9 %copy.24 = f32[512,1024]{0,1:T(8,128)} copy(f32[512,1024]{1,0:T(8,128)} %fusion.11) | data formatting | bytes 4194304 | tf_op jit(solution)/shard_map/mul | solution.py:91
  54.3 4.9 %all-to-all-start.2 = ((f32[32,512,32]{1,2,0:T(8,128)}), f32[32,512,32]{1,2,0:T(8,128)}, u32[]{:S(2)}, u32[]{:S(2)}) async-start(f32[32,512,32]{1,2,0:T(8,128)} %bitcast.26), calls=%async_computation.2 | async-start | bytes 4194304 | tf_op jit(solution)/shard_map/all_to_all | solution.py:40
  59.2 1.6 %convert_element_type.27 = f32[512,1024]{0,1:T(8,128)} convert(s32[512,1024]{0,1:T(8,128)S(1)} %copy.20) | non-fusion elementwise | flops 524288 | bytes 4194304 | tf_op jit(solution)/shard_map/convert_element_type | solution.py:67
  61.7 3.2 %fusion.1 = f32[512]{0:T(512)S(1)} fusion(f32[512,2048]{1,0:T(8,128)} %get-tuple-element.10, f32[512]{0:T(512)S(1)} %broadcast_multiply_fusion.2, f32[512]{0:T(512)S(1)} %get-tuple-element.5, f32[512]{0:T(512)S(1)} %copy-done.3), kind=kLoop, calls=%fused_computation.4 | loop fusion | flops 4193792 | bytes 4202496 | tf_op jit(solution)/shard_map/reduce_sum | solution.py:90
  64.8 19.8 %psum.21 = f32[512]{0:T(512)S(1)} all-reduce(f32[512]{0:T(512)S(1)} %fusion.1), channel_id=1, replica_groups=mesh['panel_0'=4,'panel_1'=4,'panel_2'=2,'samp'=8] {'panel_0'}, use_global_device_ids=true, to_apply=%region_7.0 | all-reduce | flops 512 | bytes 4096 | tf_op jit(solution)/shard_map/psum | solution.py:29
  84.7 8.9 %psum.22 = f32[512]{0:T(512)S(1)} all-reduce(f32[512]{0:T(512)S(1)} %psum.21), channel_id=1, replica_groups=mesh['panel_0'=4,'panel_1'=4,'panel_2'=2,'samp'=8] {'panel_1'}, use_global_device_ids=true, to_apply=%region_8.0 | all-reduce | flops 512 | bytes 4096 | tf_op jit(solution)/shard_map/psum | solution.py:29
  93.5 6.8 %psum.23 = f32[512]{0:T(512)S(1)} all-reduce(f32[512]{0:T(512)S(1)} %psum.22), channel_id=1, replica_groups=mesh['panel_0'=4,'panel_1'=4,'panel_2'=2,'samp'=8] {'panel_2'}, use_global_device_ids=true, to_apply=%region_9.0 | all-reduce | flops 512 | bytes 4096 | tf_op jit(solution)/shard_map/psum | solution.py:29
  100.3 1.7 %reduce_sum.102 = f32[512,32]{0,1:T(8,128)S(1)} reduce(f32[32,512,32]{1,2,0:T(8,128)} %all-to-all-done.2, f32[]{:T(128)} %constant.45.clone.1), dimensions={0}, to_apply=%region_5.0 | reduce | flops 507904 | bytes 2162692 | tf_op jit(solution)/shard_map/reduce_sum | solution.py:41
  102.0 1.0 multiply_reduce_fusion.1
  103.4 0.8 concatenate.3
  104.8 8.2 %all-to-all-start.3 = ((f32[8,1,369]{2,1,0:T(1,128)}), f32[8,1,369]{2,1,0:T(1,128)S(1)}, u32[]{:S(2)}, u32[]{:S(2)}) async-start(f32[8,1,369]{2,1,0:T(1,128)} %broadcast_in_dim.8), calls=%async_computation.3 | async-start | bytes 24576 | tf_op jit(solution)/shard_map/all_to_all | solution.py:14
  113.6 6.0 %all-to-all-done.3 = f32[8,1,369]{2,1,0:T(1,128)S(1)} async-done(((f32[8,1,369]{2,1,0:T(1,128)}), f32[8,1,369]{2,1,0:T(1,128)S(1)}, u32[]{:S(2)}, u32[]{:S(2)}) %all-to-all-start.3) | async-done | bytes 11840 | tf_op jit(solution)/shard_map/all_to_all | solution.py:14
  120.2 0.8 multiply_reduce_fusion.3
  122.4 0.7 fusion.17
  (27 shorter events, 3.4 us)
Async XLA Ops:
  0.6 13.5 %copy-start = (s32[512,1024]{1,0:T(8,128)S(1)}, s32[512,1024]{1,0:T(8,128)}, u32[]{:S(2)}) copy-start(s32[512,1024]{1,0:T(8,128)} %param.7) | copy-start | bytes 6291460
  5.5 16.2 %all-to-all-start = ((f32[32,1,1024]{2,1,0:T(1,128)}), f32[32,1,1024]{2,1,0:T(1,128)S(1)}, u32[]{:S(2)}, u32[]{:S(2)}) async-start(f32[32,1,1024]{2,1,0:T(1,128)} %broadcast_in_dim.6), calls=%async_computation | async-start | bytes 262144 | tf_op jit(solution)/shard_map/all_to_all | solution.py:14
  16.0 8.0 %copy-start.3 = (f32[512]{0:T(512)S(1)}, f32[512]{0:T(512)}, u32[]{:S(2)}) copy-start(f32[512]{0:T(512)} %param.9) | copy-start | bytes 6148
  54.3 6.5 %copy-start.2 = (f32[512]{0:T(512)S(1)}, f32[512]{0:T(512)}, u32[]{:S(2)}) copy-start(f32[512]{0:T(512)} %param.10) | copy-start | bytes 6148
  54.3 7.1 %copy-start.1 = (s32[512]{0:T(512)S(1)}, s32[512]{0:T(512)}, u32[]{:S(2)}) copy-start(s32[512]{0:T(512)} %param.11) | copy-start | bytes 6148
  54.3 46.0 %all-to-all-start.2 = ((f32[32,512,32]{1,2,0:T(8,128)}), f32[32,512,32]{1,2,0:T(8,128)}, u32[]{:S(2)}, u32[]{:S(2)}) async-start(f32[32,512,32]{1,2,0:T(8,128)} %bitcast.26), calls=%async_computation.2 | async-start | bytes 4194304 | tf_op jit(solution)/shard_map/all_to_all | solution.py:40
  104.8 14.8 %all-to-all-start.3 = ((f32[8,1,369]{2,1,0:T(1,128)}), f32[8,1,369]{2,1,0:T(1,128)S(1)}, u32[]{:S(2)}, u32[]{:S(2)}) async-start(f32[8,1,369]{2,1,0:T(1,128)} %broadcast_in_dim.8), calls=%async_computation.3 | async-start | bytes 24576 | tf_op jit(solution)/shard_map/all_to_all | solution.py:14
where the time goes:
time: 124 us; the launch traced here: 123 us
  blocking collectives  46.4 us (37%)
  starting transfers between devices  21.6 us (17%)
  matrix products  17.5 us (14%)
  other arithmetic  16.1 us (13%)
  waiting for transfers between devices  9.77 us (8%)
  local copies, waits for them, and re-layouts  9.63 us (8%)
  between operations  2.06 us (2%)
    psum x3, blocking collectives, over_axes(): shard = lax.psum(shard, axis)  35.4 us
    all_to_all x2, starting transfers between devices, copy_for_each(): lax.all_to_all(jnp.broadcast_to(shard[None], (count, *shard.shape)), axis...  16.8 us
    all_to_all x1, blocking collectives, copy_for_each(): lax.all_to_all(jnp.broadcast_to(shard[None], (count, *shard.shape)), axis...  11 us
    all_to_all x2, waiting for transfers between devices, copy_for_each(): lax.all_to_all(jnp.broadcast_to(shard[None], (count, *shard.shape)), axis...  9.77 us
    dot_general x1, matrix products, on_device(): jnp.dot(weights.astype(jnp.bfloat16), hap_bf, preferred_element_type=jnp....  8.51 us
    dot_general x1, matrix products, on_device(): lax.dot_general(demeaned_expected_count, hap_bf, (((1,), (1,)), ((), ()))...  7.89 us
    all_to_all x1, starting transfers between devices, sent_and_summed(): lax.all_to_all(in_blocks(shard, dim, count), axis, 0, 0, tiled=True)  4.86 us
    reduce_sum x1, other arithmetic, on_device(): allele_counts = of_everyone(jnp.sum(hap_float, axis=0), PANEL)  4.17 us
  transfers between devices with their start and end apart: 3, of which 2 were waited for; matrix products, arithmetic and copies ran while one was open for 8% of the time, Pallas kernels for 0%

commit v1 on v0

--- a/solution.py
+++ b/solution.py
@@ -26,7 +26,8 @@
 
 def over_axes(shard, axes):
     for axis in axes:
-        shard = lax.psum(shard, axis)
+        parts = lax.all_gather(shard, axis, axis=0, tiled=False)
+        shard = parts.sum(axis=0)
     return shard
 
 

time: 124 us -> 127 us (1.024)
  blocking collectives: 46.4 us -> 49.5 us
    all_gather x0 -> x3, blocking collectives: none -> 38.5 us  [over_axes(): parts = lax.all_gather(shard, axis, axis=0, tiled=False)]
    psum x3 -> x0, blocking collectives: 35.4 us -> none  [over_axes(): shard = lax.psum(shard, axis)]
where the time goes in v1:
time: 127 us; the launch traced here: 126 us
  blocking collectives  49.5 us (39%)
  starting transfers between devices  21.6 us (17%)
  matrix products  17.5 us (14%)
  other arithmetic  16.2 us (13%)
  waiting for transfers between devices  9.77 us (8%)
  local copies, waits for them, and re-layouts  9.63 us (8%)
  between operations  2.06 us (2%)
    all_gather x3, blocking collectives, over_axes(): parts = lax.all_gather(shard, axis, axis=0, tiled=False)  38.5 us
    all_to_all x2, starting transfers between devices, copy_for_each(): lax.all_to_all(jnp.broadcast_to(shard[None], (count, *shard.shape)), axis...  16.8 us
    all_to_all x1, blocking collectives, copy_for_each(): lax.all_to_all(jnp.broadcast_to(shard[None], (count, *shard.shape)), axis...  11 us
    all_to_all x2, waiting for transfers between devices, copy_for_each(): lax.all_to_all(jnp.broadcast_to(shard[None], (count, *shard.shape)), axis...  9.77 us
    dot_general x1, matrix products, on_device(): jnp.dot(weights.astype(jnp.bfloat16), hap_bf, preferred_element_type=jnp....  8.51 us
    dot_general x1, matrix products, on_device(): lax.dot_general(demeaned_expected_count, hap_bf, (((1,), (1,)), ((), ()))...  7.89 us
    all_to_all x1, starting transfers between devices, sent_and_summed(): lax.all_to_all(in_blocks(shard, dim, count), axis, 0, 0, tiled=True)  4.86 us
    reduce_sum x1, other arithmetic, on_device(): allele_counts = of_everyone(jnp.sum(hap_float, axis=0), PANEL)  4.17 us
  transfers between devices with their start and end apart: 3, of which 2 were waited for; matrix products, arithmetic and copies ran while one was open for 8% of the time, Pallas kernels for 0%

profile of v1, /device:TPU:1, one launch (start us, length us, event | category | flops | bytes accessed | tf_op | source)
XLA Modules:
  0.0 126.3 jit_solution(2019284538045139443)
XLA Ops:
  0.6 4.2 %convert_reduce_fusion = f32[1024]{0:T(1024)S(1)} fusion(s32[2048,1024]{1,0:T(8,128)} %param.8), kind=kLoop, calls=%fused_computation | loop fusion | flops 4193280 | bytes 8392704 | tf_op jit(solution)/shard_map/reduce_sum | solution.py:66
  4.8 0.7 broadcast_in_dim.6
  5.5 8.6 %all-to-all-start = ((f32[32,1,1024]{2,1,0:T(1,128)}), f32[32,1,1024]{2,1,0:T(1,128)S(1)}, u32[]{:S(2)}, u32[]{:S(2)}) async-start(f32[32,1,1024]{2,1,0:T(1,128)} %broadcast_in_dim.6), calls=%async_computation | async-start | bytes 262144 | tf_op jit(solution)/shard_map/all_to_all | solution.py:14
  14.1 1.9 %copy.23 = s32[512,1024]{0,1:T(8,128)} copy(s32[512,1024]{1,0:T(8,128)S(1)} %copy-done) | data formatting | bytes 4194304 | tf_op args[1]
  16.0 1.9 %copy.24 = s32[512,1024]{0,1:T(8,128)S(1)} copy(s32[512,1024]{1,0:T(8,128)} %param.6) | data formatting | bytes 4194304 | tf_op args[0]
  17.9 3.8 %all-to-all-done = f32[32,1,1024]{2,1,0:T(1,128)S(1)} async-done(((f32[32,1,1024]{2,1,0:T(1,128)}), f32[32,1,1024]{2,1,0:T(1,128)S(1)}, u32[]{:S(2)}, u32[]{:S(2)}) %all-to-all-start) | async-done | bytes 131104 | tf_op jit(solution)/shard_map/all_to_all | solution.py:14
  21.8 2.1 %multiply_reduce_fusion = (f32[512]{0:T(512)S(1)}, bf16[512,1024]{0,1:T(8,128)(2,1)S(1)}) fusion(f32[1024]{0:T(1024)S(1)} %get-tuple-element.8, f32[1024]{0:T(1024)S(1)} %get-tuple-element.7, s32[512,1024]{0,1:T(8,128)S(1)} %copy.24, s32[512,1024]{0,1:T(8,128)} %copy.23), kind=kLoop, calls=%fused_computation.9 | loop fusion | flops 4193792 | bytes 5253120 | tf_op jit(solution)/shard_map/reduce_sum | solution.py:73
  23.9 7.9 %fusion = (f32[512]{0:T(512)S(1)}, f32[512,2048]{1,0:T(8,128)}) fusion(f32[512]{0:T(512)S(1)} %get-tuple-element.5, f32[512]{0:T(512)S(1)} %copy-done.3, bf16[512,1024]{0,1:T(8,128)(2,1)S(1)} %get-tuple-element.6, s32[2048,1024]{1,0:T(8,128)} %param.8), kind=kOutput, calls=%fused_computation.3 | convolution fusion | flops 2152726016 | bytes 13637632 | tf_op jit(solution)/shard_map/dot_general | solution.py:77
  31.9 11.0 %all_to_all.23 = f32[32,1,512]{2,1,0:T(1,128)S(1)} all-to-all(f32[32,1,512]{2,1,0:T(1,128)S(1)} %broadcast_in_dim.7), channel_id=1, replica_groups=mesh['panel_0'=4,'panel_1'=4,'panel_2'=2,'samp'=8] {'panel_0','panel_1',..., dimensions={0} | all-to-all | bytes 131072 | tf_op jit(solution)/shard_map/all_to_all | solution.py:14
  42.9 8.5 %fusion.11 = f32[512,1024]{1,0:T(8,128)} fusion(s32[2048,1024]{1,0:T(8,128)} %param.8, f32[512,2048]{1,0:T(8,128)} %get-tuple-element.10, f32[512]{0:T(512)S(1)} %broadcast_multiply_fusion.2, f32[512]{0:T(512)S(1)} %get-tuple-element.5, f32[512]{0:T(512)S(1)} %copy-done.3), kind=kOutput, calls=%fused_computation.15 | convolution fusion | flops 2154299392 | bytes 14686208 | tf_op jit(solution)/shard_map/dot_general | solution.py:92
  51.4 2.9 %copy.28 = f32[512,1024]{0,1:T(8,128)} copy(f32[512,1024]{1,0:T(8,128)} %fusion.11) | data formatting | bytes 4194304 | tf_op jit(solution)/shard_map/mul | solution.py:92
  54.3 4.9 %all-to-all-start.2 = ((f32[32,512,32]{1,2,0:T(8,128)}), f32[32,512,32]{1,2,0:T(8,128)}, u32[]{:S(2)}, u32[]{:S(2)}) async-start(f32[32,512,32]{1,2,0:T(8,128)} %bitcast.29), calls=%async_computation.2 | async-start | bytes 4194304 | tf_op jit(solution)/shard_map/all_to_all | solution.py:41
  59.2 1.6 %convert_element_type.27 = f32[512,1024]{0,1:T(8,128)} convert(s32[512,1024]{0,1:T(8,128)S(1)} %copy.24) | non-fusion elementwise | flops 524288 | bytes 4194304 | tf_op jit(solution)/shard_map/convert_element_type | solution.py:68
  61.7 3.2 %fusion.1 = f32[512]{0:T(512)S(1)} fusion(f32[512,2048]{1,0:T(8,128)} %get-tuple-element.10, f32[512]{0:T(512)S(1)} %broadcast_multiply_fusion.2, f32[512]{0:T(512)S(1)} %get-tuple-element.5, f32[512]{0:T(512)S(1)} %copy-done.3), kind=kLoop, calls=%fused_computation.4 | loop fusion | flops 4193792 | bytes 4202496 | tf_op jit(solution)/shard_map/reduce_sum | solution.py:91
  64.8 20.6 %all-gather.3 = f32[4,1,512]{2,1,0:T(1,128)S(1)} all-gather(f32[1,1,512]{2,1,0:T(1,128)S(1)} %bitcast.30), channel_id=2, replica_groups=mesh['panel_0'=4,'panel_1'=4,'panel_2'=2,'samp'=8] {'panel_0'}, dimensions={0}, use_global_device_ids=true | all-gather | bytes 10240 | tf_op jit(solution)/shard_map/all_gather | solution.py:29
  85.4 10.9 %all-gather.4 = f32[4,1,512]{2,1,0:T(1,128)S(1)} all-gather(f32[1,1,512]{2,1,0:T(1,128)S(1)} %bitcast.33), channel_id=3, replica_groups=mesh['panel_0'=4,'panel_1'=4,'panel_2'=2,'samp'=8] {'panel_1'}, dimensions={0}, use_global_device_ids=true | all-gather | bytes 10240 | tf_op jit(solution)/shard_map/all_gather | solution.py:29
  96.4 7.0 %all-gather.5 = f32[2,1,512]{2,1,0:T(1,128)S(1)} all-gather(f32[1,1,512]{2,1,0:T(1,128)S(1)} %bitcast.34), channel_id=4, replica_groups=mesh['panel_0'=4,'panel_1'=4,'panel_2'=2,'samp'=8] {'panel_2'}, dimensions={0}, use_global_device_ids=true | all-gather | bytes 6144 | tf_op jit(solution)/shard_map/all_gather | solution.py:29
  103.5 1.7 %reduce_sum.129 = f32[512,32]{0,1:T(8,128)S(1)} reduce(f32[32,512,32]{1,2,0:T(8,128)} %all-to-all-done.2, f32[]{:T(128)} %constant.45.clone.1), dimensions={0}, to_apply=%region_5.0 | reduce | flops 507904 | bytes 2162692 | tf_op jit(solution)/shard_map/reduce_sum | solution.py:42
  105.2 1.0 multiply_reduce_fusion.1
  106.6 0.8 concatenate.3
  107.9 8.2 %all-to-all-start.3 = ((f32[8,1,369]{2,1,0:T(1,128)}), f32[8,1,369]{2,1,0:T(1,128)S(1)}, u32[]{:S(2)}, u32[]{:S(2)}) async-start(f32[8,1,369]{2,1,0:T(1,128)} %broadcast_in_dim.8), calls=%async_computation.3 | async-start | bytes 24576 | tf_op jit(solution)/shard_map/all_to_all | solution.py:14
  116.8 6.0 %all-to-all-done.3 = f32[8,1,369]{2,1,0:T(1,128)S(1)} async-done(((f32[8,1,369]{2,1,0:T(1,128)}), f32[8,1,369]{2,1,0:T(1,128)S(1)}, u32[]{:S(2)}, u32[]{:S(2)}) %all-to-all-start.3) | async-done | bytes 11840 | tf_op jit(solution)/shard_map/all_to_all | solution.py:14
  123.4 0.8 multiply_reduce_fusion.3
  125.6 0.7 fusion.17
  (30 shorter events, 3.5 us)
Async XLA Ops:
  0.6 13.5 %copy-start = (s32[512,1024]{1,0:T(8,128)S(1)}, s32[512,1024]{1,0:T(8,128)}, u32[]{:S(2)}) copy-start(s32[512,1024]{1,0:T(8,128)} %param.7) | copy-start | bytes 6291460
  5.5 16.2 %all-to-all-start = ((f32[32,1,1024]{2,1,0:T(1,128)}), f32[32,1,1024]{2,1,0:T(1,128)S(1)}, u32[]{:S(2)}, u32[]{:S(2)}) async-start(f32[32,1,1024]{2,1,0:T(1,128)} %broadcast_in_dim.6), calls=%async_computation | async-start | bytes 262144 | tf_op jit(solution)/shard_map/all_to_all | solution.py:14
  16.0 8.0 %copy-start.3 = (f32[512]{0:T(512)S(1)}, f32[512]{0:T(512)}, u32[]{:S(2)}) copy-start(f32[512]{0:T(512)} %param.9) | copy-start | bytes 6148
  54.3 6.5 %copy-start.1 = (f32[512]{0:T(512)S(1)}, f32[512]{0:T(512)}, u32[]{:S(2)}) copy-start(f32[512]{0:T(512)} %param.10) | copy-start | bytes 6148
  54.3 7.1 %copy-start.2 = (s32[512]{0:T(512)S(1)}, s32[512]{0:T(512)}, u32[]{:S(2)}) copy-start(s32[512]{0:T(512)} %param.11) | copy-start | bytes 6148
  54.3 49.1 %all-to-all-start.2 = ((f32[32,512,32]{1,2,0:T(8,128)}), f32[32,512,32]{1,2,0:T(8,128)}, u32[]{:S(2)}, u32[]{:S(2)}) async-start(f32[32,512,32]{1,2,0:T(8,128)} %bitcast.29), calls=%async_computation.2 | async-start | bytes 4194304 | tf_op jit(solution)/shard_map/all_to_all | solution.py:41
  107.9 14.8 %all-to-all-start.3 = ((f32[8,1,369]{2,1,0:T(1,128)}), f32[8,1,369]{2,1,0:T(1,128)S(1)}, u32[]{:S(2)}, u32[]{:S(2)}) async-start(f32[8,1,369]{2,1,0:T(1,128)} %broadcast_in_dim.8), calls=%async_computation.3 | async-start | bytes 24576 | tf_op jit(solution)/shard_map/all_to_all | solution.py:14
